TPU v7x, 32 devices: a whole 2x2x4 slice. The times are simulated.
32 devices in a mesh: fsdp: 32 (over z, y, x, core).
Axes of the slice: x: 2, y: 2, z: 4, core: 2. Of those that a mesh axis runs over, the one named last changes fastest.
Arguments:
- grads: bfloat16 [32, 20736, 128], P('fsdp'), may hold values from -15000 to 15000
- params: float32 [20736, 128], P('fsdp'), may hold values from -0.1875 to 0.1875
- moment: float32 [20736, 128], P('fsdp'), may hold values from -6 to 6
- second: float32 [20736, 128], P('fsdp'), may hold values from 0.1 to 4
- teacher: float32 [20736, 128], P('fsdp'), may hold values from -0.1875 to 0.1875
Outputs:
- params_out: float32 [20736, 128], P('fsdp')
- moment_out: float32 [20736, 128], P('fsdp')
- second_out: float32 [20736, 128], P('fsdp')
- teacher_out: float32 [20736, 128], P('fsdp')
- weights_out: bfloat16 [20736, 128], replicated
All inputs are finite; a program needn't handle non-finite values.
Results may differ from a plain program's by a relative error of at most 0.001.
Values may be sent and summed in bfloat16 or wider, within the bound.
A program may use at most 128 MiB of HBM per device.

v0:
```python
import functools

import jax
import jax.numpy as jnp
from jax import lax
from jax.experimental import pallas as pl
from jax.experimental.pallas import tpu as pltpu
from jax.sharding import PartitionSpec as P

MESH = pl.DeviceIdType.MESH
SHARES = (0.395, 0.765)
VMEM_GRANT = 67000000
PIECES = 8


def adamw(factor, summed, params, moment, second, teacher):
    clipped = factor * summed
    moment_out = 0.9 * moment + 0.1 * clipped
    second_out = 0.95 * second + 0.05 * clipped * clipped
    first_fix = 1.0 - 0.9**10
    second_fix = 1.0 - 0.95**10
    update = moment_out / first_fix / (jnp.sqrt(second_out / second_fix) + 1e-08) + 0.1 * params
    params_out = params - 0.001 * update
    teacher_out = 0.9999 * teacher + 0.0001 * params_out
    return params_out, moment_out, second_out, teacher_out


def plain_body(grads, params, moment, second, teacher):
    summed = lax.psum_scatter(grads[0].astype(jnp.float32), "fsdp", scatter_dimension=0, tiled=True)
    squares = lax.psum(jnp.sum(summed * summed), "fsdp")
    entries = grads.shape[1] * grads.shape[2]
    factor = 1.0 / jnp.sqrt(squares / jnp.float32(entries) + 1e-06)
    outs = adamw(factor, summed, params, moment, second, teacher)
    weights_out = lax.all_gather(outs[0].astype(jnp.bfloat16), "fsdp", axis=0, tiled=True)
    return (*outs, weights_out)


def span(masks):
    held = [0]
    for mask in masks:
        held = held + [j | mask for j in held]
    return held


def kernel(
    n, entries, parts, orders,
    grads, params, moment, second, teacher,
    params_out, moment_out, second_out, teacher_out, weights,
    state, loc, peer, *rest,
):
    n_parts = len(parts)
    sends, recvs, gathered = rest[:n_parts], rest[n_parts : 2 * n_parts], rest[2 * n_parts : 3 * n_parts]
    (total, square, squares,
     state_sem, loc_sem, peer_send, peer_recv, rs_send, rs_recv,
     sq_send, sq_recv, ag_send, ag_recv, fw_send, fw_recv, out_sem) = rest[3 * n_parts :]
    half = n // 2
    bits = n.bit_length() - 1
    me = lax.axis_index("fsdp")
    steps = [(1 << i) * (1 - 2 * ((me // (1 << i)) % 2)) for i in range(bits)]

    def at(j):
        where = me
        for i in range(bits):
            if j >> i & 1:
                where = where + steps[i]
        return where

    def remote(src, dst, send, recv, j):
        return pltpu.make_async_remote_copy(
            src_ref=src, dst_ref=dst, send_sem=send, recv_sem=recv,
            device_id=(at(j),), device_id_type=MESH,
        )

    by_need = sorted(range(half), key=lambda j: -(j & 7).bit_count() * half - j)
    peer_copies, loc_copies = {}, {}
    for j in by_need:
        peer_copies[j] = remote(grads.at[at(2 * j + 1)], peer.at[j], peer_send.at[j], peer_recv.at[j], 1)
        peer_copies[j].start()
    for j in by_need:
        loc_copies[j] = pltpu.make_async_copy(grads.at[at(2 * j)], loc.at[j], loc_sem.at[j])
        loc_copies[j].start()

    ready = set()
    rs_copies = {}

    def value(p, j, stage):
        if j not in ready:
            ready.add(j)
            loc_copies[j].wait()
            peer_copies[j].wait_recv()
        rows = pl.ds(*parts[p])
        v = loc[j, rows, :].astype(jnp.float32) + peer[j, rows, :].astype(jnp.float32)
        for mask in orders[p][:stage]:
            rs_copies[p, j | mask].wait_recv()
            v = v + recvs[p][j | mask]
        return v

    state_copies = [
        pltpu.make_async_copy(ref, state.at[i], state_sem.at[i])
        for i, ref in enumerate((params, moment, second, teacher))
    ]
    for copy in state_copies:
        copy.start()

    stages = bits - 1
    for stage in range(stages):
        todo = []
        for p in range(n_parts):
            mask, later = orders[p][stage], orders[p][stage + 1 :]
            todo.append([j | mask for j in reversed(span(later[::-1]))])
        for i in range(len(todo[0])):
            for p in range(n_parts):
                j, mask = todo[p][i], orders[p][stage]
                source, target = sends[p], recvs[p]
                source[j] = value(p, j, stage)
                rs_copies[p, j] = remote(
                    source.at[j], target.at[j], rs_send.at[p, j], rs_recv.at[p, j], 2 * mask
                )
                rs_copies[p, j].start()

    acc = jnp.zeros(square.shape, jnp.float32)
    for p in range(n_parts):
        v = value(p, 0, stages)
        total[pl.ds(*parts[p]), :] = v
        acc = acc + jnp.sum((v * v).reshape(-1, *square.shape), axis=0)
    square[...] = acc

    def square_copy(k):
        return pltpu.make_async_remote_copy(
            src_ref=square, dst_ref=squares.at[k], send_sem=sq_send.at[k], recv_sem=sq_recv.at[k],
            device_id=(lax.rem(me + k, n),), device_id_type=MESH,
        )

    @pl.loop(1, n)
    def _(k):
        square_copy(k).start()

    @pl.loop(1, n)
    def _(k):
        square_copy(k).wait()

    all_squares = square[...] + jnp.sum(squares[1:], axis=0)
    all_squares = jnp.sum(jnp.sum(all_squares, axis=0, keepdims=True), axis=1, keepdims=True)
    all_squares = jnp.broadcast_to(all_squares, (1, square.shape[1]))
    factor = 1.0 / jnp.sqrt(all_squares / jnp.float32(entries) + 1e-06)

    ag_copies, fw_copies, out_copies = {}, {}, {}

    def forward(p, j, stage):
        mask = orders[p][::-1][stage]
        ag_copies[p, j | mask] = remote(
            gathered[p].at[j], gathered[p].at[j | mask],
            ag_send.at[p, j | mask], ag_recv.at[p, j | mask], 2 * mask,
        )
        ag_copies[p, j | mask].start()

    def settle(p, j):
        rows = pl.ds(*parts[p])
        place = weights.at[at(2 * j), rows]
        fw_copies[p, j] = remote(gathered[p].at[j], place, fw_send.at[p, j], fw_recv.at[p, j], 1)
        fw_copies[p, j].start()
        out_copies[p, j] = pltpu.make_async_copy(gathered[p].at[j], place, out_sem.at[p, j])
        out_copies[p, j].start()

    for copy in state_copies:
        copy.wait()
    for p in range(n_parts):
        rows = pl.ds(*parts[p])
        outs = adamw(factor, total[rows, :], *(state[i, rows, :] for i in range(4)))
        gathered[p][0] = outs[0].astype(jnp.bfloat16)
        forward(p, 0, 0)
        params_out[rows, :], moment_out[rows, :], second_out[rows, :], teacher_out[rows, :] = outs
    for stage in range(1, stages):
        for p in range(n_parts):
            forward(p, 0, stage)
    for p in range(n_parts):
        settle(p, 0)
    for stage in range(stages):
        for i in range(1 << stage):
            for p in range(n_parts):
                order = orders[p][::-1]
                j = span(order[:stage])[i] | order[stage]
                ag_copies[p, j].wait_recv()
                for later in range(stage + 1, stages):
                    forward(p, j, later)
                settle(p, j)

    for copy in fw_copies.values():
        copy.wait()
    for copy in out_copies.values():
        copy.wait()
    for copies in (peer_copies, rs_copies, ag_copies):
        for copy in copies.values():
            copy.wait_send()


def land(*refs):
    sources, places, held, (in_sem, out_sem) = refs[:5], refs[5:10], refs[10:15], refs[15:]
    jobs = [(i, pl.ds(0, sources[i].shape[0])) for i in range(4)]
    size = sources[4].shape[0] // PIECES // 16 * 16
    for k in range(PIECES):
        jobs.append((4, pl.ds(k * size, size if k < PIECES - 1 else sources[4].shape[0] - k * size)))
    jobs = jobs[4:] + jobs[:4]
    incoming = [
        pltpu.make_async_copy(sources[i].at[rows], held[i].at[rows], in_sem.at[k])
        for k, (i, rows) in enumerate(jobs)
    ]
    outgoing = [
        pltpu.make_async_copy(held[i].at[rows], places[i].at[rows], out_sem.at[k])
        for k, (i, rows) in enumerate(jobs)
    ]
    for copy in incoming:
        copy.start()
    for copy, out in zip(incoming, outgoing):
        copy.wait()
        out.start()
    for out in outgoing:
        out.wait()


def split(rows):
    first = int(rows * SHARES[0]) // 16 * 16
    second = int(rows * SHARES[1]) // 16 * 16
    return ((0, first), (first, second - first), (second, rows - second))


def fast_body(n, grads, params, moment, second, teacher):
    rows, lanes = params.shape
    half = n // 2
    parts = split(rows)
    masks = [1 << i for i in range(n.bit_length() - 2)]
    orders = (
        tuple(masks),
        (masks[1], masks[0], *masks[2:]),
        (*masks[2:], masks[0], masks[1]),
    )
    shard = jax.ShapeDtypeStruct((rows, lanes), jnp.float32)
    vmem, hbm, anywhere = (pl.BlockSpec(memory_space=space) for space in (pltpu.VMEM, pltpu.HBM, pl.ANY))
    narrow, wide = ([pltpu.VMEM((half, size, lanes), t) for _, size in parts] for t in (jnp.bfloat16, jnp.float32))
    dma = pltpu.SemaphoreType.DMA
    per_part = dma((len(parts), half))
    outs = pl.pallas_call(
        functools.partial(kernel, n, grads.shape[1] * lanes, parts, orders),
        out_shape=(shard,) * 4 + (jax.ShapeDtypeStruct((n, rows, lanes), jnp.bfloat16),),
        in_specs=[anywhere] + [hbm] * 4,
        out_specs=(vmem,) * 4 + (anywhere,),
        scratch_shapes=[pltpu.VMEM((4, rows, lanes), jnp.float32)]
        + [pltpu.VMEM((half, rows, lanes), jnp.bfloat16)] * 2
        + wide + wide + narrow
        + [
            pltpu.VMEM((rows, lanes), jnp.float32),
            pltpu.VMEM((8, lanes), jnp.float32),
            pltpu.VMEM((n, 8, lanes), jnp.float32),
            dma((4,)), dma((half,)), dma((half,)), dma((half,)),
            per_part, per_part,
            dma((n,)), dma((n,)),
            per_part, per_part, per_part, per_part, per_part,
        ],
        compiler_params=pltpu.CompilerParams(has_side_effects=True, vmem_limit_bytes=VMEM_GRANT),
    )(grads.reshape(n, rows, lanes), params, moment, second, teacher)
    shapes = (shard,) * 4 + (jax.ShapeDtypeStruct((n * rows, lanes), jnp.bfloat16),)
    return pl.pallas_call(
        land,
        out_shape=shapes,
        in_specs=[anywhere] * 5,
        out_specs=(anywhere,) * 5,
        scratch_shapes=[pltpu.VMEM(s.shape, s.dtype) for s in shapes] + [dma((4 + PIECES,))] * 2,
        compiler_params=pltpu.CompilerParams(vmem_limit_bytes=VMEM_GRANT),
    )(*outs[:4], outs[4].reshape(n * rows, lanes))


def body(n, grads, params, moment, second, teacher):
    if n & (n - 1) == 0 and 16 <= n <= 64 and params.shape[0] % 8 == 0 and params.shape[0] >= 128:
        return fast_body(n, grads, params, moment, second, teacher)
    return plain_body(grads, params, moment, second, teacher)


def solution(mesh):
    in_specs = (
        P("fsdp", None, None),
        P("fsdp", None),
        P("fsdp", None),
        P("fsdp", None),
        P("fsdp", None),
    )
    out_specs = (P("fsdp", None), P("fsdp", None), P("fsdp", None), P("fsdp", None), P())
    run = functools.partial(body, mesh.shape["fsdp"])
    return jax.shard_map(run, mesh=mesh, in_specs=in_specs, out_specs=out_specs, check_vma=False)
```

profile of v0, /device:TPU:0, one launch (start us, length us, event | category | flops | bytes accessed | tf_op | source)
XLA Modules:
  0.0 94.1 jit_solution(17771883334353230043)
XLA Ops:
  0.6 88.0 %shard_map.92 = (f32[648,128]{1,0:T(8,128)}, f32[648,128]{1,0:T(8,128)}, f32[648,128]{1,0:T(8,128)}, f32[648,128]{1,0:T(8,128)}, bf16[32,648,128]{2,1,0:T(8,128)(2,1)}) custom-call(bf16[32,648,128]{2,1,0:T(8,128)(2,1)} %bitcast.2, f32[648,128]{1,0:T(8,128)} %params.1, f32[648,128]{1,0:T(8,128)} %moment.1, f32[648,128]{1,0:T(8,128)} %second.1, f32[648,128]{1,0:T(8,128)} %teacher.1), custom_call_target="tpu_custom_call" | custom-call | tf_op jit(solution)/shard_map/pallas_call | solution.py:242
  88.6 5.5 %shard_map.93 = (f32[648,128]{1,0:T(8,128)}, f32[648,128]{1,0:T(8,128)}, f32[648,128]{1,0:T(8,128)}, f32[648,128]{1,0:T(8,128)}, bf16[20736,128]{1,0:T(8,128)(2,1)}) custom-call(f32[648,128]{1,0:T(8,128)} %get-tuple-element.10.refs_0_, f32[648,128]{1,0:T(8,128)} %get-tuple-element.11.refs_1_, f32[648,128]{1,0:T(8,128)} %get-tuple-element.12.refs_2_, ...), custom_call_target="tpu_custom_call" | custom-call | tf_op jit(solution)/shard_map/pallas_call | solution.py:262
where the time goes:
time: 94.2 us; the launch traced here: 94.1 us
  Pallas kernels  93.5 us (99%)
    pallas_call x1, Pallas kernels, fast_body(): pl.pallas_call(functools.partial(kernel, n, grads.shape[1] * lanes, parts...  88 us
    pallas_call x1, Pallas kernels, fast_body(): pl.pallas_call(land, out_shape=shapes, in_specs=[anywhere] * 5, out_specs...  5.48 us

commit v1 on v0

--- a/solution.py
+++ b/solution.py
@@ -11,6 +11,8 @@
 SHARES = (0.395, 0.765)
 VMEM_GRANT = 67000000
 PIECES = 8
+NARROW_SCALE = 2.0**12
+NARROW_FLOOR = 2.0**-125
 
 
 def adamw(factor, summed, params, moment, second, teacher):
@@ -23,6 +25,18 @@
     params_out = params - 0.001 * update
     teacher_out = 0.9999 * teacher + 0.0001 * params_out
     return params_out, moment_out, second_out, teacher_out
+
+
+def narrowed(v):
+    v = v * NARROW_SCALE
+    return (v * jnp.abs(v) * (v * v)).astype(jnp.bfloat16)
+
+
+def widened(x):
+    x = x.astype(jnp.float32)
+    for _ in range(2):
+        x = x * lax.rsqrt(jnp.maximum(jnp.abs(x), NARROW_FLOOR))
+    return x * (1.0 / NARROW_SCALE)
 
 
 def plain_body(grads, params, moment, second, teacher):
@@ -92,7 +106,7 @@
         v = loc[j, rows, :].astype(jnp.float32) + peer[j, rows, :].astype(jnp.float32)
         for mask in orders[p][:stage]:
             rs_copies[p, j | mask].wait_recv()
-            v = v + recvs[p][j | mask]
+            v = v + widened(recvs[p][j | mask])
         return v
 
     state_copies = [
@@ -112,7 +126,7 @@
             for p in range(n_parts):
                 j, mask = todo[p][i], orders[p][stage]
                 source, target = sends[p], recvs[p]
-                source[j] = value(p, j, stage)
+                source[j] = narrowed(value(p, j, stage))
                 rs_copies[p, j] = remote(
                     source.at[j], target.at[j], rs_send.at[p, j], rs_recv.at[p, j], 2 * mask
                 )
@@ -236,7 +250,7 @@
     )
     shard = jax.ShapeDtypeStruct((rows, lanes), jnp.float32)
     vmem, hbm, anywhere = (pl.BlockSpec(memory_space=space) for space in (pltpu.VMEM, pltpu.HBM, pl.ANY))
-    narrow, wide = ([pltpu.VMEM((half, size, lanes), t) for _, size in parts] for t in (jnp.bfloat16, jnp.float32))
+    narrow = [pltpu.VMEM((half, size, lanes), jnp.bfloat16) for _, size in parts]
     dma = pltpu.SemaphoreType.DMA
     per_part = dma((len(parts), half))
     outs = pl.pallas_call(
@@ -246,7 +260,7 @@
         out_specs=(vmem,) * 4 + (anywhere,),
         scratch_shapes=[pltpu.VMEM((4, rows, lanes), jnp.float32)]
         + [pltpu.VMEM((half, rows, lanes), jnp.bfloat16)] * 2
-        + wide + wide + narrow
+        + narrow * 3
         + [
             pltpu.VMEM((rows, lanes), jnp.float32),
             pltpu.VMEM((8, lanes), jnp.float32),

time: 94.2 us -> 75.9 us (0.81)
  Pallas kernels: 93.5 us -> 75.2 us
    pallas_call x1, Pallas kernels: 88 us -> 69.7 us  [fast_body(): pl.pallas_call(functools.partial(kernel, n, grads.shape[1] * lanes, parts...]
where the time goes in v1:
time: 75.9 us; the launch traced here: 75.8 us
  Pallas kernels  75.2 us (99%)
    pallas_call x1, Pallas kernels, fast_body(): pl.pallas_call(functools.partial(kernel, n, grads.shape[1] * lanes, parts...  69.7 us
    pallas_call x1, Pallas kernels, fast_body(): pl.pallas_call(land, out_shape=shapes, in_specs=[anywhere] * 5, out_specs...  5.48 us

profile of v1, /device:TPU:0, one launch (start us, length us, event | category | flops | bytes accessed | tf_op | source)
XLA Modules:
  0.0 75.8 jit_solution(3042224961516026598)
XLA Ops:
  0.6 69.7 %shard_map.92 = (f32[648,128]{1,0:T(8,128)}, f32[648,128]{1,0:T(8,128)}, f32[648,128]{1,0:T(8,128)}, f32[648,128]{1,0:T(8,128)}, bf16[32,648,128]{2,1,0:T(8,128)(2,1)}) custom-call(bf16[32,648,128]{2,1,0:T(8,128)(2,1)} %bitcast.2, f32[648,128]{1,0:T(8,128)} %params.1, f32[648,128]{1,0:T(8,128)} %moment.1, f32[648,128]{1,0:T(8,128)} %second.1, f32[648,128]{1,0:T(8,128)} %teacher.1), custom_call_target="tpu_custom_call" | custom-call | tf_op jit(solution)/shard_map/pallas_call | solution.py:256
  70.3 5.5 %shard_map.93 = (f32[648,128]{1,0:T(8,128)}, f32[648,128]{1,0:T(8,128)}, f32[648,128]{1,0:T(8,128)}, f32[648,128]{1,0:T(8,128)}, bf16[20736,128]{1,0:T(8,128)(2,1)}) custom-call(f32[648,128]{1,0:T(8,128)} %get-tuple-element.10.refs_0_, f32[648,128]{1,0:T(8,128)} %get-tuple-element.11.refs_1_, f32[648,128]{1,0:T(8,128)} %get-tuple-element.12.refs_2_, ...), custom_call_target="tpu_custom_call" | custom-call | tf_op jit(solution)/shard_map/pallas_call | solution.py:276

commit v2 on v1

--- a/solution.py
+++ b/solution.py
@@ -9,8 +9,8 @@
 
 MESH = pl.DeviceIdType.MESH
 SHARES = (0.395, 0.765)
-VMEM_GRANT = 67000000
-PIECES = 8
+VMEM_GRANT = 40000000
+PIECES = 4
 NARROW_SCALE = 2.0**12
 NARROW_FLOOR = 2.0**-125
 
@@ -63,10 +63,10 @@
     state, loc, peer, *rest,
 ):
     n_parts = len(parts)
-    sends, recvs, gathered = rest[:n_parts], rest[n_parts : 2 * n_parts], rest[2 * n_parts : 3 * n_parts]
+    sends, recvs = rest[:n_parts], rest[n_parts : 2 * n_parts]
     (total, square, squares,
      state_sem, loc_sem, peer_send, peer_recv, rs_send, rs_recv,
-     sq_send, sq_recv, ag_send, ag_recv, fw_send, fw_recv, out_sem) = rest[3 * n_parts :]
+     sq_send, sq_recv, ag_send, ag_recv, fw_send, fw_recv) = rest[2 * n_parts :]
     half = n // 2
     bits = n.bit_length() - 1
     me = lax.axis_index("fsdp")
@@ -85,14 +85,19 @@
             device_id=(at(j),), device_id_type=MESH,
         )
 
+    barrier = pltpu.get_barrier_semaphore()
+    for i in range(bits):
+        pl.semaphore_signal(barrier, inc=1, device_id=(at(1 << i),), device_id_type=MESH)
+
     by_need = sorted(range(half), key=lambda j: -(j & 7).bit_count() * half - j)
     peer_copies, loc_copies = {}, {}
     for j in by_need:
+        loc_copies[j] = pltpu.make_async_copy(grads.at[at(2 * j)], loc.at[j], loc_sem.at[j])
+        loc_copies[j].start()
+    pl.semaphore_wait(barrier, bits)
+    for j in by_need:
         peer_copies[j] = remote(grads.at[at(2 * j + 1)], peer.at[j], peer_send.at[j], peer_recv.at[j], 1)
         peer_copies[j].start()
-    for j in by_need:
-        loc_copies[j] = pltpu.make_async_copy(grads.at[at(2 * j)], loc.at[j], loc_sem.at[j])
-        loc_copies[j].start()
 
     ready = set()
     rs_copies = {}
@@ -158,30 +163,28 @@
     all_squares = jnp.broadcast_to(all_squares, (1, square.shape[1]))
     factor = 1.0 / jnp.sqrt(all_squares / jnp.float32(entries) + 1e-06)
 
-    ag_copies, fw_copies, out_copies = {}, {}, {}
+    ag_copies, fw_copies = {}, {}
+
+    def place(p, j):
+        return weights.at[at(2 * j), pl.ds(*parts[p])]
 
     def forward(p, j, stage):
         mask = orders[p][::-1][stage]
         ag_copies[p, j | mask] = remote(
-            gathered[p].at[j], gathered[p].at[j | mask],
-            ag_send.at[p, j | mask], ag_recv.at[p, j | mask], 2 * mask,
+            place(p, j), place(p, j), ag_send.at[p, j | mask], ag_recv.at[p, j | mask], 2 * mask
         )
         ag_copies[p, j | mask].start()
 
     def settle(p, j):
-        rows = pl.ds(*parts[p])
-        place = weights.at[at(2 * j), rows]
-        fw_copies[p, j] = remote(gathered[p].at[j], place, fw_send.at[p, j], fw_recv.at[p, j], 1)
+        fw_copies[p, j] = remote(place(p, j), place(p, j), fw_send.at[p, j], fw_recv.at[p, j], 1)
         fw_copies[p, j].start()
-        out_copies[p, j] = pltpu.make_async_copy(gathered[p].at[j], place, out_sem.at[p, j])
-        out_copies[p, j].start()
 
     for copy in state_copies:
         copy.wait()
     for p in range(n_parts):
         rows = pl.ds(*parts[p])
         outs = adamw(factor, total[rows, :], *(state[i, rows, :] for i in range(4)))
-        gathered[p][0] = outs[0].astype(jnp.bfloat16)
+        weights[me, rows, :] = outs[0].astype(jnp.bfloat16)
         forward(p, 0, 0)
         params_out[rows, :], moment_out[rows, :], second_out[rows, :], teacher_out[rows, :] = outs
     for stage in range(1, stages):
@@ -201,32 +204,23 @@
 
     for copy in fw_copies.values():
         copy.wait()
-    for copy in out_copies.values():
-        copy.wait()
     for copies in (peer_copies, rs_copies, ag_copies):
         for copy in copies.values():
             copy.wait_send()
 
 
 def land(*refs):
-    sources, places, held, (in_sem, out_sem) = refs[:5], refs[5:10], refs[10:15], refs[15:]
-    jobs = [(i, pl.ds(0, sources[i].shape[0])) for i in range(4)]
-    size = sources[4].shape[0] // PIECES // 16 * 16
+    held, places, out_sem = refs[:5], refs[5:10], refs[10]
+    size = held[4].shape[0] // PIECES // 16 * 16
+    jobs = []
     for k in range(PIECES):
-        jobs.append((4, pl.ds(k * size, size if k < PIECES - 1 else sources[4].shape[0] - k * size)))
-    jobs = jobs[4:] + jobs[:4]
-    incoming = [
-        pltpu.make_async_copy(sources[i].at[rows], held[i].at[rows], in_sem.at[k])
-        for k, (i, rows) in enumerate(jobs)
-    ]
+        jobs.append((4, pl.ds(k * size, size if k < PIECES - 1 else held[4].shape[0] - k * size)))
+    jobs += [(i, pl.ds(0, held[i].shape[0])) for i in range(4)]
     outgoing = [
         pltpu.make_async_copy(held[i].at[rows], places[i].at[rows], out_sem.at[k])
         for k, (i, rows) in enumerate(jobs)
     ]
-    for copy in incoming:
-        copy.start()
-    for copy, out in zip(incoming, outgoing):
-        copy.wait()
+    for out in outgoing:
         out.start()
     for out in outgoing:
         out.wait()
@@ -248,19 +242,18 @@
         (masks[1], masks[0], *masks[2:]),
         (*masks[2:], masks[0], masks[1]),
     )
-    shard = jax.ShapeDtypeStruct((rows, lanes), jnp.float32)
-    vmem, hbm, anywhere = (pl.BlockSpec(memory_space=space) for space in (pltpu.VMEM, pltpu.HBM, pl.ANY))
+    vmem, hbm = (pl.BlockSpec(memory_space=space) for space in (pltpu.VMEM, pltpu.HBM))
     narrow = [pltpu.VMEM((half, size, lanes), jnp.bfloat16) for _, size in parts]
     dma = pltpu.SemaphoreType.DMA
     per_part = dma((len(parts), half))
     outs = pl.pallas_call(
         functools.partial(kernel, n, grads.shape[1] * lanes, parts, orders),
-        out_shape=(shard,) * 4 + (jax.ShapeDtypeStruct((n, rows, lanes), jnp.bfloat16),),
-        in_specs=[anywhere] + [hbm] * 4,
-        out_specs=(vmem,) * 4 + (anywhere,),
+        out_shape=(pltpu.VMEM((rows, lanes), jnp.float32),) * 4 + (pltpu.VMEM((n, rows, lanes), jnp.bfloat16),),
+        in_specs=[hbm] * 5,
+        out_specs=(vmem,) * 5,
         scratch_shapes=[pltpu.VMEM((4, rows, lanes), jnp.float32)]
         + [pltpu.VMEM((half, rows, lanes), jnp.bfloat16)] * 2
-        + narrow * 3
+        + narrow * 2
         + [
             pltpu.VMEM((rows, lanes), jnp.float32),
             pltpu.VMEM((8, lanes), jnp.float32),
@@ -268,19 +261,21 @@
             dma((4,)), dma((half,)), dma((half,)), dma((half,)),
             per_part, per_part,
             dma((n,)), dma((n,)),
-            per_part, per_part, per_part, per_part, per_part,
+            per_part, per_part, per_part, per_part,
         ],
-        compiler_params=pltpu.CompilerParams(has_side_effects=True, vmem_limit_bytes=VMEM_GRANT),
-    )(grads.reshape(n, rows, lanes), params, moment, second, teacher)
-    shapes = (shard,) * 4 + (jax.ShapeDtypeStruct((n * rows, lanes), jnp.bfloat16),)
+        compiler_params=pltpu.CompilerParams(
+            collective_id=0, has_side_effects=True, vmem_limit_bytes=VMEM_GRANT
+        ),
+    )(*(pltpu.with_memory_space_constraint(x, pltpu.HBM) for x in (grads.reshape(n, rows, lanes), params, moment, second, teacher)))
+    held = [pltpu.with_memory_space_constraint(x, pltpu.VMEM) for x in (*outs[:4], outs[4].reshape(n * rows, lanes))]
     return pl.pallas_call(
         land,
-        out_shape=shapes,
-        in_specs=[anywhere] * 5,
-        out_specs=(anywhere,) * 5,
-        scratch_shapes=[pltpu.VMEM(s.shape, s.dtype) for s in shapes] + [dma((4 + PIECES,))] * 2,
+        out_shape=tuple(jax.ShapeDtypeStruct(x.shape, x.dtype) for x in held),
+        in_specs=[vmem] * 5,
+        out_specs=(hbm,) * 5,
+        scratch_shapes=[dma((4 + PIECES,))],
         compiler_params=pltpu.CompilerParams(vmem_limit_bytes=VMEM_GRANT),
-    )(*outs[:4], outs[4].reshape(n * rows, lanes))
+    )(*held)
 
 
 def body(n, grads, params, moment, second, teacher):

time: 75.9 us -> 67.5 us (0.89)
  Pallas kernels: 75.2 us -> 66.7 us
    pallas_call x1, Pallas kernels: 69.7 us -> 63.8 us  [fast_body(): pl.pallas_call(functools.partial(kernel, n, grads.shape[1] * lanes, parts...]
    pallas_call x1, Pallas kernels: 5.48 us -> 2.84 us  [fast_body(): pl.pallas_call(land, out_shape=tuple((jax.ShapeDtypeStruct(x.shape, x.dty...]
where the time goes in v2:
time: 67.5 us; the launch traced here: 67.3 us
  Pallas kernels  66.7 us (99%)
    pallas_call x1, Pallas kernels, fast_body(): pl.pallas_call(functools.partial(kernel, n, grads.shape[1] * lanes, parts...  63.8 us
    pallas_call x1, Pallas kernels, fast_body(): pl.pallas_call(land, out_shape=tuple((jax.ShapeDtypeStruct(x.shape, x.dty...  2.84 us

profile of v2, /device:TPU:0, one launch (start us, length us, event | category | flops | bytes accessed | tf_op | source)
XLA Modules:
  0.0 67.3 jit_solution(9408674756990203616)
XLA Ops:
  0.6 63.8 %shard_map.92 = (f32[648,128]{1,0:T(8,128)S(1)}, f32[648,128]{1,0:T(8,128)S(1)}, f32[648,128]{1,0:T(8,128)S(1)}, f32[648,128]{1,0:T(8,128)S(1)}, bf16[32,648,128]{2,1,0:T(8,128)(2,1)S(1)}) custom-call(bf16[32,648,128]{2,1,0:T(8,128)(2,1)} %bitcast.3, f32[648,128]{1,0:T(8,128)} %params.1, f32[648,128]{1,0:T(8,128)} %moment.1, f32[648,128]{1,0:T(8,128)} %second.1, ...), custom_call_target="tpu_custom_call" | custom-call | tf_op jit(solution)/shard_map/pallas_call | solution.py:249
  64.5 2.8 %shard_map.93 = (f32[648,128]{1,0:T(8,128)}, f32[648,128]{1,0:T(8,128)}, f32[648,128]{1,0:T(8,128)}, f32[648,128]{1,0:T(8,128)}, bf16[20736,128]{1,0:T(8,128)(2,1)}) custom-call(f32[648,128]{1,0:T(8,128)S(1)} %get-tuple-element.10.refs_0_, f32[648,128]{1,0:T(8,128)S(1)} %get-tuple-element.11.refs_1_, f32[648,128]{1,0:T(8,128)S(1)} %get-tuple-element.12.refs_2_, ...), custom_call_target="tpu_custom_call" | custom-call | tf_op jit(solution)/shard_map/pallas_call | solution.py:271

commit v3 on v2

v3 whole, which is shorter than its diff:
```python
import functools

import jax
import jax.numpy as jnp
from jax import lax
from jax.experimental import pallas as pl
from jax.experimental.pallas import tpu as pltpu
from jax.sharding import PartitionSpec as P

MESH = pl.DeviceIdType.MESH
PLAN = (
    ("01z", 0.195), ("10z", 0.195), ("z01", 0.11),
    ("01z", 0.195), ("10z", 0.195), ("z10", 0.11),
)
VMEM_GRANT = 40000000
PIECES = 4
RS_WEIGHTS = (1.0, 1.0, 1.3, 1.8, 1.0)
AG_WEIGHTS = (1.0, 1.0, 1.0, 1.0, 1.0)
NARROW_SCALE = 2.0**12
NARROW_FLOOR = 2.0**-125


def adamw(factor, summed, params, moment, second, teacher):
    clipped = factor * summed
    moment_out = 0.9 * moment + 0.1 * clipped
    second_out = 0.95 * second + 0.05 * clipped * clipped
    first_fix = 1.0 - 0.9**10
    second_fix = 1.0 - 0.95**10
    update = moment_out / first_fix / (jnp.sqrt(second_out / second_fix) + 1e-08) + 0.1 * params
    params_out = params - 0.001 * update
    teacher_out = 0.9999 * teacher + 0.0001 * params_out
    return params_out, moment_out, second_out, teacher_out


def narrowed(v):
    v = v * NARROW_SCALE
    return (v * jnp.abs(v) * (v * v)).astype(jnp.bfloat16)


def widened(x):
    x = x.astype(jnp.float32)
    for _ in range(2):
        x = x * lax.rsqrt(jnp.maximum(jnp.abs(x), NARROW_FLOOR))
    return x * (1.0 / NARROW_SCALE)


def plain_body(grads, params, moment, second, teacher):
    summed = lax.psum_scatter(grads[0].astype(jnp.float32), "fsdp", scatter_dimension=0, tiled=True)
    squares = lax.psum(jnp.sum(summed * summed), "fsdp")
    entries = grads.shape[1] * grads.shape[2]
    factor = 1.0 / jnp.sqrt(squares / jnp.float32(entries) + 1e-06)
    outs = adamw(factor, summed, params, moment, second, teacher)
    weights_out = lax.all_gather(outs[0].astype(jnp.bfloat16), "fsdp", axis=0, tiled=True)
    return (*outs, weights_out)


def first_of(order, j):
    return next(i for i, mask in enumerate(order) if j & mask)


def kernel(
    n, entries, parts, orders,
    grads, params, moment, second, teacher,
    params_out, moment_out, second_out, teacher_out, weights,
    state, pairs, *rest,
):
    n_parts = len(parts)
    sends, recvs = rest[:n_parts], rest[n_parts : 2 * n_parts]
    (total, square, squares,
     state_sem, pair_sem, recv_sem, peer_send, rs_send, ag_send, fw_send, fw_recv,
     sq_send, sq_recv) = rest[2 * n_parts :]
    half = n // 2
    bits = n.bit_length() - 1
    me = lax.axis_index("fsdp")
    steps = [(1 << i) * (1 - 2 * ((me // (1 << i)) % 2)) for i in range(bits)]

    def at(j):
        where = me
        for i in range(bits):
            if j >> i & 1:
                where = where + steps[i]
        return where

    def remote(src, dst, send, recv, j):
        pltpu.make_async_remote_copy(
            src_ref=src, dst_ref=dst, send_sem=send, recv_sem=recv,
            device_id=(at(j),), device_id_type=MESH,
        ).start()

    def settled(ref, sem):
        pltpu.make_async_copy(ref, ref, sem).wait()

    barrier = pltpu.get_barrier_semaphore()
    for i in range(bits):
        pl.semaphore_signal(barrier, inc=1, device_id=(at(1 << i),), device_id_type=MESH)

    by_need = sorted(range(half), key=lambda j: (-j.bit_count(), -j))
    for j in by_need:
        pltpu.make_async_copy(grads.at[at(2 * j)], pairs.at[j, 0], pair_sem.at[j]).start()
    for i, ref in enumerate((params, moment, second, teacher)):
        pltpu.make_async_copy(ref, state.at[i], state_sem).start()
    pl.semaphore_wait(barrier, bits)
    for j in by_need:
        remote(grads.at[at(2 * j + 1)], pairs.at[j, 1], peer_send, pair_sem.at[j], 1)

    ready = set()

    def value(p, j, stage):
        if j not in ready:
            ready.add(j)
            settled(pairs.at[j], pair_sem.at[j])
        rows = pl.ds(*parts[p])
        v = pairs[j, 0, rows, :].astype(jnp.float32) + pairs[j, 1, rows, :].astype(jnp.float32)
        for mask in orders[p][:stage]:
            settled(recvs[p].at[j | mask], recv_sem.at[p, j | mask])
            v = v + widened(recvs[p][j | mask])
        return v

    def haul(weigh, j):
        return sum(weigh[i] for i in range(half.bit_length()) if j >> i & 1)

    def rs_key(t):
        return -haul(RS_WEIGHTS, t[1]), t[2], -t[1], t[0]

    def ag_key(t):
        return haul(AG_WEIGHTS, t[1]), -t[2], t[1], t[0]

    stages = bits - 1
    todo = [(p, j, first_of(orders[p], j)) for p in range(n_parts) for j in range(1, half)]
    for p, j, stage in sorted(todo, key=rs_key):
        sends[p][j] = narrowed(value(p, j, stage))
        remote(sends[p].at[j], recvs[p].at[j], rs_send, recv_sem.at[p, j], 2 * orders[p][stage])

    acc = jnp.zeros((8, square.shape[1]), jnp.float32)
    for p in range(n_parts):
        v = value(p, 0, stages)
        total[pl.ds(*parts[p]), :] = v
        acc = acc + jnp.sum((v * v).reshape(-1, *acc.shape), axis=0)
    square[...] = jnp.sum(acc, axis=0, keepdims=True)

    @pl.loop(1, n)
    def _(k):
        pltpu.make_async_remote_copy(
            src_ref=square, dst_ref=squares.at[k], send_sem=sq_send, recv_sem=sq_recv,
            device_id=(lax.rem(me + k, n),), device_id_type=MESH,
        ).start()

    settled(state, state_sem)
    settled(squares.at[1:], sq_recv)
    all_squares = square[...] + jnp.sum(squares[1:], axis=0)
    all_squares = jnp.sum(all_squares, axis=1, keepdims=True)
    all_squares = jnp.broadcast_to(all_squares, (1, square.shape[1]))
    factor = 1.0 / jnp.sqrt(all_squares / jnp.float32(entries) + 1e-06)

    def place(p, j):
        return weights.at[at(2 * j), pl.ds(*parts[p])]

    def onward(p, j):
        for mask in orders[p][: first_of(orders[p], j) if j else stages][::-1]:
            remote(place(p, j), place(p, j), ag_send, recv_sem.at[p, j | mask], 2 * mask)
        remote(place(p, j), place(p, j), fw_send, fw_recv, 1)

    for p in range(n_parts):
        rows = pl.ds(*parts[p])
        outs = adamw(factor, total[rows, :], *(state[i, rows, :] for i in range(4)))
        weights[me, rows, :] = outs[0].astype(jnp.bfloat16)
        onward(p, 0)
        params_out[rows, :], moment_out[rows, :], second_out[rows, :], teacher_out[rows, :] = outs
    for p, j, stage in sorted(todo, key=ag_key):
        settled(place(p, j), recv_sem.at[p, j])
        onward(p, j)

    settled(weights.at[:half], fw_recv)
    settled(weights.at[:half], fw_send)
    settled(weights.at[:half], peer_send)
    settled(weights.at[: half - 1], rs_send)
    settled(weights.at[: half - 1], ag_send)
    settled(squares.at[1:], sq_send)


def land(*refs):
    held, places, out_sem = refs[:5], refs[5:10], refs[10]
    size = held[4].shape[0] // PIECES // 16 * 16
    jobs = []
    for k in range(PIECES):
        jobs.append((4, pl.ds(k * size, size if k < PIECES - 1 else held[4].shape[0] - k * size)))
    jobs += [(i, pl.ds(0, held[i].shape[0])) for i in range(4)]
    outgoing = [
        pltpu.make_async_copy(held[i].at[rows], places[i].at[rows], out_sem.at[k])
        for k, (i, rows) in enumerate(jobs)
    ]
    for out in outgoing:
        out.start()
    for out in outgoing:
        out.wait()


def split(rows):
    ends, share = [0], 0.0
    for _, part in PLAN[:-1]:
        share += part
        ends.append(int(rows * share) // 16 * 16)
    return tuple((lo, hi - lo) for lo, hi in zip(ends, ends[1:] + [rows]))


def fast_body(n, grads, params, moment, second, teacher):
    rows, lanes = params.shape
    half = n // 2
    parts = split(rows)
    masks = [1 << i for i in range(n.bit_length() - 2)]
    axes = {"0": masks[:1], "1": masks[1:2], "z": masks[2:]}
    orders = tuple(tuple(mask for axis in plan for mask in axes[axis]) for plan, _ in PLAN)
    vmem, hbm = (pl.BlockSpec(memory_space=space) for space in (pltpu.VMEM, pltpu.HBM))
    narrow = [pltpu.VMEM((half, size, lanes), jnp.bfloat16) for _, size in parts]
    dma = pltpu.SemaphoreType.DMA
    outs = pl.pallas_call(
        functools.partial(kernel, n, grads.shape[1] * lanes, parts, orders),
        out_shape=(pltpu.VMEM((rows, lanes), jnp.float32),) * 4 + (pltpu.VMEM((n, rows, lanes), jnp.bfloat16),),
        in_specs=[hbm] * 5,
        out_specs=(vmem,) * 5,
        scratch_shapes=[pltpu.VMEM((4, rows, lanes), jnp.float32)]
        + [pltpu.VMEM((half, 2, rows, lanes), jnp.bfloat16)]
        + narrow * 2
        + [
            pltpu.VMEM((rows, lanes), jnp.float32),
            pltpu.VMEM((1, lanes), jnp.float32),
            pltpu.VMEM((n, 1, lanes), jnp.float32),
            dma, dma((half,)), dma((len(parts), half)), dma, dma, dma, dma, dma, dma, dma,
        ],
        compiler_params=pltpu.CompilerParams(
            collective_id=0, has_side_effects=True, vmem_limit_bytes=VMEM_GRANT
        ),
    )(*(pltpu.with_memory_space_constraint(x, pltpu.HBM) for x in (grads.reshape(n, rows, lanes), params, moment, second, teacher)))
    held = [pltpu.with_memory_space_constraint(x, pltpu.VMEM) for x in (*outs[:4], outs[4].reshape(n * rows, lanes))]
    return pl.pallas_call(
        land,
        out_shape=tuple(jax.ShapeDtypeStruct(x.shape, x.dtype) for x in held),
        in_specs=[vmem] * 5,
        out_specs=(hbm,) * 5,
        scratch_shapes=[dma((4 + PIECES,))],
        compiler_params=pltpu.CompilerParams(vmem_limit_bytes=VMEM_GRANT),
    )(*held)


def body(n, grads, params, moment, second, teacher):
    if n & (n - 1) == 0 and 16 <= n <= 64 and params.shape[0] % 8 == 0 and params.shape[0] >= 128:
        return fast_body(n, grads, params, moment, second, teacher)
    return plain_body(grads, params, moment, second, teacher)


def solution(mesh):
    in_specs = (
        P("fsdp", None, None),
        P("fsdp", None),
        P("fsdp", None),
        P("fsdp", None),
        P("fsdp", None),
    )
    out_specs = (P("fsdp", None), P("fsdp", None), P("fsdp", None), P("fsdp", None), P())
    run = functools.partial(body, mesh.shape["fsdp"])
    return jax.shard_map(run, mesh=mesh, in_specs=in_specs, out_specs=out_specs, check_vma=False)
```

time: 67.5 us -> 60 us (0.89)
  Pallas kernels: 66.7 us -> 59.2 us
    pallas_call x1, Pallas kernels: 63.8 us -> 56.3 us  [fast_body(): pl.pallas_call(functools.partial(kernel, n, grads.shape[1] * lanes, parts...]
where the time goes in v3:
time: 60 us; the launch traced here: 59.8 us
  Pallas kernels  59.2 us (99%)
  between operations  0.64 us (1%)
    pallas_call x1, Pallas kernels, fast_body(): pl.pallas_call(functools.partial(kernel, n, grads.shape[1] * lanes, parts...  56.3 us
    pallas_call x1, Pallas kernels, fast_body(): pl.pallas_call(land, out_shape=tuple((jax.ShapeDtypeStruct(x.shape, x.dty...  2.84 us

profile of v3, /device:TPU:0, one launch (start us, length us, event | category | flops | bytes accessed | tf_op | source)
XLA Modules:
  0.0 59.8 jit_solution(14497694636172509721)
XLA Ops:
  0.6 56.3 %shard_map.92 = (f32[648,128]{1,0:T(8,128)S(1)}, f32[648,128]{1,0:T(8,128)S(1)}, f32[648,128]{1,0:T(8,128)S(1)}, f32[648,128]{1,0:T(8,128)S(1)}, bf16[32,648,128]{2,1,0:T(8,128)(2,1)S(1)}) custom-call(bf16[32,648,128]{2,1,0:T(8,128)(2,1)} %bitcast.3, f32[648,128]{1,0:T(8,128)} %params.1, f32[648,128]{1,0:T(8,128)} %moment.1, f32[648,128]{1,0:T(8,128)} %second.1, ...), custom_call_target="tpu_custom_call" | custom-call | tf_op jit(solution)/shard_map/pallas_call | solution.py:216
  57.0 2.8 %shard_map.93 = (f32[648,128]{1,0:T(8,128)}, f32[648,128]{1,0:T(8,128)}, f32[648,128]{1,0:T(8,128)}, f32[648,128]{1,0:T(8,128)}, bf16[20736,128]{1,0:T(8,128)(2,1)}) custom-call(f32[648,128]{1,0:T(8,128)S(1)} %get-tuple-element.10.refs_0_, f32[648,128]{1,0:T(8,128)S(1)} %get-tuple-element.11.refs_1_, f32[648,128]{1,0:T(8,128)S(1)} %get-tuple-element.12.refs_2_, ...), custom_call_target="tpu_custom_call" | custom-call | tf_op jit(solution)/shard_map/pallas_call | solution.py:235

commit v4 on v3

--- a/solution.py
+++ b/solution.py
@@ -9,8 +9,8 @@
 
 MESH = pl.DeviceIdType.MESH
 PLAN = (
-    ("01z", 0.195), ("10z", 0.195), ("z01", 0.11),
-    ("01z", 0.195), ("10z", 0.195), ("z10", 0.11),
+    ("01z", 0.1977), ("10z", 0.1977), ("z01", 0.099),
+    ("01z", 0.1977), ("10z", 0.1977), ("z10", 0.1113),
 )
 VMEM_GRANT = 40000000
 PIECES = 4
@@ -18,6 +18,29 @@
 AG_WEIGHTS = (1.0, 1.0, 1.0, 1.0, 1.0)
 NARROW_SCALE = 2.0**12
 NARROW_FLOOR = 2.0**-125
+FAR_WEIGHTS = (1.0, 1.0, 1.0, 2.0, 2.0)
+RS_ORDER = (
+    (1, 15), (3, 15), (2, 15), (5, 14), (5, 13), (5, 15), (2, 13), (0, 15), (4, 15), (4, 11),
+    (2, 12), (1, 14), (3, 11), (2, 7), (1, 11), (0, 11), (0, 9), (2, 11), (5, 5), (5, 7),
+    (1, 7), (1, 13), (0, 7), (4, 7), (0, 13), (4, 13), (2, 4), (2, 14), (5, 11), (5, 12),
+    (5, 6), (4, 10), (4, 14), (2, 9), (1, 10), (5, 4), (1, 9), (4, 9), (3, 13), (3, 7),
+    (0, 5), (0, 14), (2, 3), (3, 14), (1, 3), (2, 8), (2, 5), (1, 12), (3, 3), (5, 8),
+    (4, 6), (2, 6), (2, 10), (5, 9), (4, 12), (1, 5), (3, 5), (0, 6), (0, 10), (5, 10),
+    (3, 10), (3, 9), (0, 12), (1, 6), (3, 12), (0, 3), (2, 1), (4, 3), (1, 8), (4, 8),
+    (0, 4), (4, 5), (3, 6), (5, 3), (0, 1), (1, 2), (1, 1), (0, 8), (2, 2), (3, 2),
+    (1, 4), (3, 1), (3, 8), (4, 1), (0, 2), (3, 4), (4, 2), (5, 2), (5, 1), (4, 4),
+)
+AG_ORDER = (
+    (0, 2), (1, 1), (0, 4), (2, 2), (3, 2), (0, 8), (1, 4), (4, 1), (1, 2), (1, 8),
+    (3, 8), (3, 4), (4, 8), (5, 1), (0, 6), (2, 1), (1, 3), (1, 10), (4, 4), (1, 9),
+    (0, 12), (1, 12), (3, 9), (1, 6), (5, 2), (1, 5), (0, 1), (5, 3), (2, 3), (3, 12),
+    (4, 12), (2, 5), (2, 8), (2, 10), (0, 7), (3, 3), (4, 3), (4, 6), (0, 10), (3, 1),
+    (3, 10), (4, 5), (4, 9), (1, 13), (5, 9), (3, 6), (0, 13), (2, 9), (1, 11), (0, 14),
+    (5, 10), (3, 14), (5, 4), (5, 8), (4, 2), (5, 7), (5, 11), (3, 5), (5, 5), (2, 4),
+    (4, 13), (2, 11), (0, 3), (2, 14), (4, 10), (1, 7), (0, 9), (3, 7), (5, 6), (2, 6),
+    (0, 11), (3, 13), (0, 5), (4, 11), (4, 7), (5, 12), (5, 13), (1, 15), (2, 13), (5, 14),
+    (4, 14), (2, 7), (2, 12), (5, 15), (1, 14), (3, 15), (3, 11), (4, 15), (0, 15), (2, 15),
+)
 
 
 def adamw(factor, summed, params, moment, second, teacher):
@@ -125,9 +148,14 @@
     def ag_key(t):
         return haul(AG_WEIGHTS, t[1]), -t[2], t[1], t[0]
 
+    def arranged(order, key):
+        if len(order) != len(todo):
+            return sorted(todo, key=key)
+        return [(p, j, first_of(orders[p], j)) for p, j in order]
+
     stages = bits - 1
     todo = [(p, j, first_of(orders[p], j)) for p in range(n_parts) for j in range(1, half)]
-    for p, j, stage in sorted(todo, key=rs_key):
+    for p, j, stage in arranged(RS_ORDER, rs_key):
         sends[p][j] = narrowed(value(p, j, stage))
         remote(sends[p].at[j], recvs[p].at[j], rs_send, recv_sem.at[p, j], 2 * orders[p][stage])
 
@@ -138,12 +166,8 @@
         acc = acc + jnp.sum((v * v).reshape(-1, *acc.shape), axis=0)
     square[...] = jnp.sum(acc, axis=0, keepdims=True)
 
-    @pl.loop(1, n)
-    def _(k):
-        pltpu.make_async_remote_copy(
-            src_ref=square, dst_ref=squares.at[k], send_sem=sq_send, recv_sem=sq_recv,
-            device_id=(lax.rem(me + k, n),), device_id_type=MESH,
-        ).start()
+    for k in sorted(range(1, n), key=lambda k: -haul(FAR_WEIGHTS, k >> 1) - (k & 1) / n):
+        remote(square, squares.at[k], sq_send, sq_recv, k)
 
     settled(state, state_sem)
     settled(squares.at[1:], sq_recv)
@@ -166,7 +190,7 @@
         weights[me, rows, :] = outs[0].astype(jnp.bfloat16)
         onward(p, 0)
         params_out[rows, :], moment_out[rows, :], second_out[rows, :], teacher_out[rows, :] = outs
-    for p, j, stage in sorted(todo, key=ag_key):
+    for p, j, stage in arranged(AG_ORDER, ag_key):
         settled(place(p, j), recv_sem.at[p, j])
         onward(p, j)
 

time: 60 us -> 57.4 us (0.957)
  Pallas kernels: 59.2 us -> 56.6 us
    pallas_call x1, Pallas kernels: 56.3 us -> 53.7 us  [fast_body(): pl.pallas_call(functools.partial(kernel, n, grads.shape[1] * lanes, parts...]
where the time goes in v4:
time: 57.4 us; the launch traced here: 57.2 us
  Pallas kernels  56.6 us (99%)
  between operations  0.64 us (1%)
    pallas_call x1, Pallas kernels, fast_body(): pl.pallas_call(functools.partial(kernel, n, grads.shape[1] * lanes, parts...  53.7 us
    pallas_call x1, Pallas kernels, fast_body(): pl.pallas_call(land, out_shape=tuple((jax.ShapeDtypeStruct(x.shape, x.dty...  2.84 us

profile of v4, /device:TPU:0, one launch (start us, length us, event | category | flops | bytes accessed | tf_op | source)
XLA Modules:
  0.0 57.2 jit_solution(898054439737044379)
XLA Ops:
  0.6 53.7 %shard_map.92 = (f32[648,128]{1,0:T(8,128)S(1)}, f32[648,128]{1,0:T(8,128)S(1)}, f32[648,128]{1,0:T(8,128)S(1)}, f32[648,128]{1,0:T(8,128)S(1)}, bf16[32,648,128]{2,1,0:T(8,128)(2,1)S(1)}) custom-call(bf16[32,648,128]{2,1,0:T(8,128)(2,1)} %bitcast.3, f32[648,128]{1,0:T(8,128)} %params.1, f32[648,128]{1,0:T(8,128)} %moment.1, f32[648,128]{1,0:T(8,128)} %second.1, ...), custom_call_target="tpu_custom_call" | custom-call | tf_op jit(solution)/shard_map/pallas_call | solution.py:240
  54.4 2.8 %shard_map.93 = (f32[648,128]{1,0:T(8,128)}, f32[648,128]{1,0:T(8,128)}, f32[648,128]{1,0:T(8,128)}, f32[648,128]{1,0:T(8,128)}, bf16[20736,128]{1,0:T(8,128)(2,1)}) custom-call(f32[648,128]{1,0:T(8,128)S(1)} %get-tuple-element.10.refs_0_, f32[648,128]{1,0:T(8,128)S(1)} %get-tuple-element.11.refs_1_, f32[648,128]{1,0:T(8,128)S(1)} %get-tuple-element.12.refs_2_, ...), custom_call_target="tpu_custom_call" | custom-call | tf_op jit(solution)/shard_map/pallas_call | solution.py:259

commit v5 on v4

--- a/solution.py
+++ b/solution.py
@@ -9,8 +9,8 @@
 
 MESH = pl.DeviceIdType.MESH
 PLAN = (
-    ("01z", 0.1977), ("10z", 0.1977), ("z01", 0.099),
-    ("01z", 0.1977), ("10z", 0.1977), ("z10", 0.1113),
+    ("01z", 0.2224), ("10z", 0.2224), ("z01", 0.099),
+    ("01z", 0.173), ("10z", 0.173), ("z10", 0.1113),
 )
 VMEM_GRANT = 40000000
 PIECES = 4
@@ -20,26 +20,26 @@
 NARROW_FLOOR = 2.0**-125
 FAR_WEIGHTS = (1.0, 1.0, 1.0, 2.0, 2.0)
 RS_ORDER = (
-    (1, 15), (3, 15), (2, 15), (5, 14), (5, 13), (5, 15), (2, 13), (0, 15), (4, 15), (4, 11),
-    (2, 12), (1, 14), (3, 11), (2, 7), (1, 11), (0, 11), (0, 9), (2, 11), (5, 5), (5, 7),
-    (1, 7), (1, 13), (0, 7), (4, 7), (0, 13), (4, 13), (2, 4), (2, 14), (5, 11), (5, 12),
-    (5, 6), (4, 10), (4, 14), (2, 9), (1, 10), (5, 4), (1, 9), (4, 9), (3, 13), (3, 7),
-    (0, 5), (0, 14), (2, 3), (3, 14), (1, 3), (2, 8), (2, 5), (1, 12), (3, 3), (5, 8),
-    (4, 6), (2, 6), (2, 10), (5, 9), (4, 12), (1, 5), (3, 5), (0, 6), (0, 10), (5, 10),
-    (3, 10), (3, 9), (0, 12), (1, 6), (3, 12), (0, 3), (2, 1), (4, 3), (1, 8), (4, 8),
-    (0, 4), (4, 5), (3, 6), (5, 3), (0, 1), (1, 2), (1, 1), (0, 8), (2, 2), (3, 2),
-    (1, 4), (3, 1), (3, 8), (4, 1), (0, 2), (3, 4), (4, 2), (5, 2), (5, 1), (4, 4),
+    (2, 15), (0, 15), (4, 15), (1, 15), (2, 14), (4, 14), (5, 15), (0, 13), (5, 7), (3, 15),
+    (0, 7), (0, 11), (5, 13), (5, 14), (2, 7), (1, 11), (2, 13), (4, 11), (5, 12), (2, 11),
+    (1, 14), (4, 13), (2, 10), (3, 11), (5, 5), (5, 11), (0, 14), (1, 13), (2, 12), (5, 9),
+    (4, 3), (3, 7), (2, 6), (1, 7), (3, 13), (4, 7), (5, 10), (4, 9), (2, 4), (3, 5),
+    (4, 10), (2, 5), (3, 14), (4, 12), (5, 8), (0, 10), (0, 12), (0, 9), (2, 8), (1, 10),
+    (1, 9), (2, 3), (2, 9), (3, 10), (1, 6), (3, 6), (1, 5), (0, 6), (1, 12), (0, 5),
+    (5, 4), (3, 9), (4, 8), (3, 12), (0, 8), (5, 6), (0, 3), (3, 3), (4, 5), (1, 3),
+    (4, 6), (1, 8), (5, 3), (0, 1), (1, 4), (3, 1), (2, 1), (1, 2), (4, 1), (2, 2),
+    (4, 2), (3, 8), (3, 4), (0, 2), (0, 4), (1, 1), (3, 2), (4, 4), (5, 2), (5, 1),
 )
 AG_ORDER = (
-    (0, 2), (1, 1), (0, 4), (2, 2), (3, 2), (0, 8), (1, 4), (4, 1), (1, 2), (1, 8),
-    (3, 8), (3, 4), (4, 8), (5, 1), (0, 6), (2, 1), (1, 3), (1, 10), (4, 4), (1, 9),
-    (0, 12), (1, 12), (3, 9), (1, 6), (5, 2), (1, 5), (0, 1), (5, 3), (2, 3), (3, 12),
-    (4, 12), (2, 5), (2, 8), (2, 10), (0, 7), (3, 3), (4, 3), (4, 6), (0, 10), (3, 1),
-    (3, 10), (4, 5), (4, 9), (1, 13), (5, 9), (3, 6), (0, 13), (2, 9), (1, 11), (0, 14),
-    (5, 10), (3, 14), (5, 4), (5, 8), (4, 2), (5, 7), (5, 11), (3, 5), (5, 5), (2, 4),
-    (4, 13), (2, 11), (0, 3), (2, 14), (4, 10), (1, 7), (0, 9), (3, 7), (5, 6), (2, 6),
-    (0, 11), (3, 13), (0, 5), (4, 11), (4, 7), (5, 12), (5, 13), (1, 15), (2, 13), (5, 14),
-    (4, 14), (2, 7), (2, 12), (5, 15), (1, 14), (3, 15), (3, 11), (4, 15), (0, 15), (2, 15),
+    (1, 1), (0, 2), (0, 4), (0, 8), (1, 4), (3, 2), (4, 1), (1, 8), (3, 8), (5, 1),
+    (3, 4), (3, 1), (4, 8), (5, 2), (2, 2), (0, 6), (2, 4), (4, 4), (1, 6), (0, 12),
+    (0, 3), (1, 12), (2, 1), (3, 12), (5, 3), (4, 9), (0, 9), (0, 5), (3, 3), (1, 5),
+    (4, 12), (5, 5), (2, 3), (1, 9), (4, 5), (1, 2), (3, 10), (0, 14), (2, 8), (5, 8),
+    (0, 7), (3, 9), (4, 6), (0, 10), (5, 9), (1, 3), (1, 13), (3, 6), (2, 10), (2, 9),
+    (5, 10), (2, 6), (1, 14), (4, 2), (0, 1), (3, 5), (5, 6), (5, 11), (3, 14), (4, 11),
+    (3, 13), (4, 13), (5, 7), (2, 11), (2, 5), (1, 7), (4, 7), (5, 4), (0, 13), (5, 14),
+    (3, 11), (5, 13), (0, 11), (5, 12), (2, 12), (2, 13), (1, 11), (1, 15), (2, 7), (1, 10),
+    (2, 14), (0, 15), (3, 7), (4, 14), (4, 10), (5, 15), (4, 3), (3, 15), (4, 15), (2, 15),
 )
 
 
@@ -126,6 +126,9 @@
     for j in by_need:
         remote(grads.at[at(2 * j + 1)], pairs.at[j, 1], peer_send, pair_sem.at[j], 1)
 
+    def slot(p, j):
+        return [k for k in range(half) if not k & orders[p][0]].index(j)
+
     ready = set()
 
     def value(p, j, stage):
@@ -134,8 +137,9 @@
             settled(pairs.at[j], pair_sem.at[j])
         rows = pl.ds(*parts[p])
         v = pairs[j, 0, rows, :].astype(jnp.float32) + pairs[j, 1, rows, :].astype(jnp.float32)
+        if stage:
+            settled(recvs[p].at[:stage], recv_sem.at[p, slot(p, j)])
         for mask in orders[p][:stage]:
-            settled(recvs[p].at[j | mask], recv_sem.at[p, j | mask])
             v = v + widened(recvs[p][j | mask])
         return v
 
@@ -157,7 +161,8 @@
     todo = [(p, j, first_of(orders[p], j)) for p in range(n_parts) for j in range(1, half)]
     for p, j, stage in arranged(RS_ORDER, rs_key):
         sends[p][j] = narrowed(value(p, j, stage))
-        remote(sends[p].at[j], recvs[p].at[j], rs_send, recv_sem.at[p, j], 2 * orders[p][stage])
+        mask = orders[p][stage]
+        remote(sends[p].at[j], recvs[p].at[j], rs_send, recv_sem.at[p, slot(p, j ^ mask)], 2 * mask)
 
     acc = jnp.zeros((8, square.shape[1]), jnp.float32)
     for p in range(n_parts):
@@ -176,12 +181,21 @@
     all_squares = jnp.broadcast_to(all_squares, (1, square.shape[1]))
     factor = 1.0 / jnp.sqrt(all_squares / jnp.float32(entries) + 1e-06)
 
+    arrivals = arranged(AG_ORDER, ag_key)
+    leaves = [[j for q, j, stage in arrivals if q == p and not stage] for p in range(n_parts)]
+
+    def landing(p, j):
+        if j not in leaves[p]:
+            return recv_sem.at[p, slot(p, j)]
+        pair = leaves[p].index(j) // 2
+        return recv_sem.at[p, half // 2 - 1 + pair if pair else 0]
+
     def place(p, j):
         return weights.at[at(2 * j), pl.ds(*parts[p])]
 
     def onward(p, j):
         for mask in orders[p][: first_of(orders[p], j) if j else stages][::-1]:
-            remote(place(p, j), place(p, j), ag_send, recv_sem.at[p, j | mask], 2 * mask)
+            remote(place(p, j), place(p, j), ag_send, landing(p, j | mask), 2 * mask)
         remote(place(p, j), place(p, j), fw_send, fw_recv, 1)
 
     for p in range(n_parts):
@@ -190,9 +204,14 @@
         weights[me, rows, :] = outs[0].astype(jnp.bfloat16)
         onward(p, 0)
         params_out[rows, :], moment_out[rows, :], second_out[rows, :], teacher_out[rows, :] = outs
-    for p, j, stage in arranged(AG_ORDER, ag_key):
-        settled(place(p, j), recv_sem.at[p, j])
-        onward(p, j)
+    for p, j, stage in arrivals:
+        if stage:
+            settled(place(p, j), landing(p, j))
+            onward(p, j)
+        elif leaves[p].index(j) % 2:
+            settled(recvs[p].at[:2], landing(p, j))
+            onward(p, leaves[p][leaves[p].index(j) - 1])
+            onward(p, j)
 
     settled(weights.at[:half], fw_recv)
     settled(weights.at[:half], fw_send)
@@ -249,7 +268,7 @@
             pltpu.VMEM((rows, lanes), jnp.float32),
             pltpu.VMEM((1, lanes), jnp.float32),
             pltpu.VMEM((n, 1, lanes), jnp.float32),
-            dma, dma((half,)), dma((len(parts), half)), dma, dma, dma, dma, dma, dma, dma,
+            dma, dma((half,)), dma((len(parts), half // 2 + half // 4 - 1)), dma, dma, dma, dma, dma, dma, dma,
         ],
         compiler_params=pltpu.CompilerParams(
             collective_id=0, has_side_effects=True, vmem_limit_bytes=VMEM_GRANT

time: 57.4 us -> 56.7 us (0.988)
  Pallas kernels: 56.6 us -> 55.9 us
    pallas_call x1, Pallas kernels: 53.7 us -> 53 us  [fast_body(): pl.pallas_call(functools.partial(kernel, n, grads.shape[1] * lanes, parts...]
where the time goes in v5:
time: 56.7 us; the launch traced here: 56.5 us
  Pallas kernels  55.9 us (99%)
  between operations  0.64 us (1%)
    pallas_call x1, Pallas kernels, fast_body(): pl.pallas_call(functools.partial(kernel, n, grads.shape[1] * lanes, parts...  53 us
    pallas_call x1, Pallas kernels, fast_body(): pl.pallas_call(land, out_shape=tuple((jax.ShapeDtypeStruct(x.shape, x.dty...  2.84 us

profile of v5, /device:TPU:0, one launch (start us, length us, event | category | flops | bytes accessed | tf_op | source)
XLA Modules:
  0.0 56.5 jit_solution(7459485032249421451)
XLA Ops:
  0.6 53.0 %shard_map.92 = (f32[648,128]{1,0:T(8,128)S(1)}, f32[648,128]{1,0:T(8,128)S(1)}, f32[648,128]{1,0:T(8,128)S(1)}, f32[648,128]{1,0:T(8,128)S(1)}, bf16[32,648,128]{2,1,0:T(8,128)(2,1)S(1)}) custom-call(bf16[32,648,128]{2,1,0:T(8,128)(2,1)} %bitcast.3, f32[648,128]{1,0:T(8,128)} %params.1, f32[648,128]{1,0:T(8,128)} %moment.1, f32[648,128]{1,0:T(8,128)} %second.1, ...), custom_call_target="tpu_custom_call" | custom-call | tf_op jit(solution)/shard_map/pallas_call | solution.py:259
  53.7 2.8 %shard_map.93 = (f32[648,128]{1,0:T(8,128)}, f32[648,128]{1,0:T(8,128)}, f32[648,128]{1,0:T(8,128)}, f32[648,128]{1,0:T(8,128)}, bf16[20736,128]{1,0:T(8,128)(2,1)}) custom-call(f32[648,128]{1,0:T(8,128)S(1)} %get-tuple-element.10.refs_0_, f32[648,128]{1,0:T(8,128)S(1)} %get-tuple-element.11.refs_1_, f32[648,128]{1,0:T(8,128)S(1)} %get-tuple-element.12.refs_2_, ...), custom_call_target="tpu_custom_call" | custom-call | tf_op jit(solution)/shard_map/pallas_call | solution.py:278

commit v6 on v5

--- a/solution.py
+++ b/solution.py
@@ -91,7 +91,7 @@
     sends, recvs = rest[:n_parts], rest[n_parts : 2 * n_parts]
     (total, square, squares,
      state_sem, pair_sem, recv_sem, peer_send, rs_send, ag_send, fw_send, fw_recv,
-     sq_send, sq_recv) = rest[2 * n_parts :]
+     sq_send, sq_recv, relay) = rest[2 * n_parts :]
     half = n // 2
     bits = n.bit_length() - 1
     me = lax.axis_index("fsdp")
@@ -114,22 +114,41 @@
         pltpu.make_async_copy(ref, ref, sem).wait()
 
     barrier = pltpu.get_barrier_semaphore()
-    for i in range(bits):
-        pl.semaphore_signal(barrier, inc=1, device_id=(at(1 << i),), device_id_type=MESH)
+    lined = bits == 5
+    greeted = [at(1 << i) for i in range(bits - lined)]
+    inner = 0
+    if lined:
+        level = me // (n // 4)
+        inner = (level + 1) // 2 % 2
+        near = me + (3 - 2 * level) * (n // 4)
+
+    def greet(sem, where):
+        pl.semaphore_signal(sem, inc=1, device_id=(where,), device_id_type=MESH)
+
+    for where in greeted:
+        greet(barrier, where)
+    if lined:
+        pl.when(inner == 1)(lambda: greet(barrier, near))
 
     by_need = sorted(range(half), key=lambda j: (-j.bit_count(), -j))
     for j in by_need:
         pltpu.make_async_copy(grads.at[at(2 * j)], pairs.at[j, 0], pair_sem.at[j]).start()
     for i, ref in enumerate((params, moment, second, teacher)):
         pltpu.make_async_copy(ref, state.at[i], state_sem).start()
-    pl.semaphore_wait(barrier, bits)
+    pl.semaphore_wait(barrier, len(greeted) + inner)
     for j in by_need:
         remote(grads.at[at(2 * j + 1)], pairs.at[j, 1], peer_send, pair_sem.at[j], 1)
 
     def slot(p, j):
         return [k for k in range(half) if not k & orders[p][0]].index(j)
 
-    ready = set()
+    ready, relayed = set(), []
+
+    if lined:
+        @pl.when(inner == 1)
+        def _():
+            greet(relay, greeted[-1])
+            greet(relay, near)
 
     def value(p, j, stage):
         if j not in ready:
@@ -161,6 +180,9 @@
     todo = [(p, j, first_of(orders[p], j)) for p in range(n_parts) for j in range(1, half)]
     for p, j, stage in arranged(RS_ORDER, rs_key):
         sends[p][j] = narrowed(value(p, j, stage))
+        if lined and orders[p][stage] == half // 2 and not relayed:
+            relayed.append(True)
+            pl.semaphore_wait(relay, 1)
         mask = orders[p][stage]
         remote(sends[p].at[j], recvs[p].at[j], rs_send, recv_sem.at[p, slot(p, j ^ mask)], 2 * mask)
 
@@ -269,6 +291,7 @@
             pltpu.VMEM((1, lanes), jnp.float32),
             pltpu.VMEM((n, 1, lanes), jnp.float32),
             dma, dma((half,)), dma((len(parts), half // 2 + half // 4 - 1)), dma, dma, dma, dma, dma, dma, dma,
+            pltpu.SemaphoreType.REGULAR,
         ],
         compiler_params=pltpu.CompilerParams(
             collective_id=0, has_side_effects=True, vmem_limit_bytes=VMEM_GRANT

time: 56.7 us -> 56.3 us (level)
  no operation moved by 1% of the time
where the time goes in v6:
time: 56.3 us; the launch traced here: 56.2 us
  Pallas kernels  55.5 us (99%)
  between operations  0.64 us (1%)
    pallas_call x1, Pallas kernels, fast_body(): pl.pallas_call(functools.partial(kernel, n, grads.shape[1] * lanes, parts...  52.7 us
    pallas_call x1, Pallas kernels, fast_body(): pl.pallas_call(land, out_shape=tuple((jax.ShapeDtypeStruct(x.shape, x.dty...  2.84 us

profile of v6, /device:TPU:0, one launch (start us, length us, event | category | flops | bytes accessed | tf_op | source)
XLA Modules:
  0.0 56.2 jit_solution(14270376112681105388)
XLA Ops:
  0.6 52.7 %shard_map.92 = (f32[648,128]{1,0:T(8,128)S(1)}, f32[648,128]{1,0:T(8,128)S(1)}, f32[648,128]{1,0:T(8,128)S(1)}, f32[648,128]{1,0:T(8,128)S(1)}, bf16[32,648,128]{2,1,0:T(8,128)(2,1)S(1)}) custom-call(bf16[32,648,128]{2,1,0:T(8,128)(2,1)} %bitcast.3, f32[648,128]{1,0:T(8,128)} %params.1, f32[648,128]{1,0:T(8,128)} %moment.1, f32[648,128]{1,0:T(8,128)} %second.1, ...), custom_call_target="tpu_custom_call" | custom-call | tf_op jit(solution)/shard_map/pallas_call | solution.py:281
  53.3 2.8 %shard_map.93 = (f32[648,128]{1,0:T(8,128)}, f32[648,128]{1,0:T(8,128)}, f32[648,128]{1,0:T(8,128)}, f32[648,128]{1,0:T(8,128)}, bf16[20736,128]{1,0:T(8,128)(2,1)}) custom-call(f32[648,128]{1,0:T(8,128)S(1)} %get-tuple-element.10.refs_0_, f32[648,128]{1,0:T(8,128)S(1)} %get-tuple-element.11.refs_1_, f32[648,128]{1,0:T(8,128)S(1)} %get-tuple-element.12.refs_2_, ...), custom_call_target="tpu_custom_call" | custom-call | tf_op jit(solution)/shard_map/pallas_call | solution.py:301
